TPU v7x, 32 devices: a whole 2x2x4 slice. The times are simulated.
32 devices in a mesh: fsdp: 8 (over z, y), tensor: 4 (over x, core).
Axes of the slice: x: 2, y: 2, z: 4, core: 2. Of those that a mesh axis runs over, the one named last changes fastest.
Arguments:
- activations: bfloat16 [8192, 5120], P('fsdp', 'tensor'), may hold values from -6 to 6
- cotangent: bfloat16 [8192, 5120], P('fsdp', 'tensor'), may hold values from -0.06591797 to 0.06591797
- weights: float32 [5120, 5120], P(None, ('tensor', 'fsdp')), may hold values from -0.025 to 0.025
- first_moment: float32 [5120, 5120], P(None, ('tensor', 'fsdp')), may hold values from -3 to 3
- second_moment: float32 [5120, 5120], P(None, ('tensor', 'fsdp')), may hold values from 0.01 to 1
Outputs:
- weights_new: float32 [5120, 5120], P('fsdp', 'tensor')
- first_new: float32 [5120, 5120], P('fsdp', 'tensor')
- second_new: float32 [5120, 5120], P('fsdp', 'tensor')
- weights_bf16: bfloat16 [5120, 5120], P(None, 'tensor')
All inputs are finite; a program needn't handle non-finite values.
Results may differ from a plain program's by a relative error of at most 0.014.
Values may be sent and summed in bfloat16 or wider, within the bound.
A program may use at most 128 MiB of HBM per device.

v0:
```python
import functools

import jax
import jax.numpy as jnp
from jax import lax
from jax.experimental import pallas as pl
from jax.experimental.pallas import tpu as pltpu
from jax.sharding import PartitionSpec as P


STEP = 20


beta_one = 0.9
beta_two = 0.95
adam_eps = 1e-08
learn_rate = 0.0003
decay_rate = 0.1


def adam_update(weights, first_moment, second_moment, gradient):
    first_new = beta_one * first_moment + (1.0 - beta_one) * gradient
    second_new = beta_two * second_moment + (1.0 - beta_two) * gradient * gradient
    corrected = first_new / (1.0 - beta_one**STEP)
    scaled = jnp.sqrt(second_new / (1.0 - beta_two**STEP)) + adam_eps
    weights_new = weights - learn_rate * (corrected / scaled + decay_rate * weights)
    return (weights_new, first_new, second_new)


def line_pairs(length, step, senders):
    return [
        (2 * z + p, 2 * (z + step) + p)
        for z in range(length)
        for p in range(2)
        if senders(z) and 0 <= z + step < length
    ]


def reduce_line(term, z, length):
    last = length - 1
    right = left = None
    for s in range(last):
        up = term(jnp.clip(last + z - s, 0, last))
        down = term(jnp.clip(s - last + z, 0, last))
        if s:
            up = (up.astype(jnp.float32) + right.astype(jnp.float32)).astype(jnp.bfloat16)
            down = (down.astype(jnp.float32) + left.astype(jnp.float32)).astype(jnp.bfloat16)
        right = lax.ppermute(up, "fsdp", line_pairs(length, 1, lambda i: i <= s))
        left = lax.ppermute(down, "fsdp", line_pairs(length, -1, lambda i: i >= last - s))
    own = term(z)
    own = own.astype(jnp.float32)
    if last:
        own = own + right.astype(jnp.float32) + left.astype(jnp.float32)
    return own


def gather_kernel(
    length, own_ref, out_ref, local_sem, y_send, y_recv, r_send, r_recv, l_send, l_recv
):
    f = lax.axis_index("fsdp")
    z, p = f // 2, f % 2
    last = length - 1
    rows = own_ref.shape[0]
    pair, right, left = f + 1 - 2 * p, f + 2, f - 2

    def block(c):
        return out_ref.at[pl.ds((2 * c + p) * rows, rows)]

    def copy(src, dst, send, recv, target):
        return pltpu.make_async_remote_copy(
            src_ref=src,
            dst_ref=dst,
            send_sem=send,
            recv_sem=recv,
            device_id={"fsdp": target},
            device_id_type=pl.DeviceIdType.MESH,
        )

    def to_pair(c, src=None):
        return copy(block(c) if src is None else src, block(c), y_send.at[c], y_recv.at[c], pair)

    def to_right(s, src=None):
        c = z - s
        return copy(block(c) if src is None else src, block(c), r_send.at[s], r_recv.at[s], right)

    def to_left(s, src=None):
        c = z + s
        return copy(block(c) if src is None else src, block(c), l_send.at[s], l_recv.at[s], left)

    barrier = pltpu.get_barrier_semaphore()
    pl.semaphore_signal(
        barrier, inc=1, device_id={"fsdp": pair}, device_id_type=pl.DeviceIdType.MESH
    )

    @pl.when(z > 0)
    def _():
        pl.semaphore_signal(
            barrier, inc=1, device_id={"fsdp": left}, device_id_type=pl.DeviceIdType.MESH
        )

    @pl.when(z < last)
    def _():
        pl.semaphore_signal(
            barrier, inc=1, device_id={"fsdp": right}, device_id_type=pl.DeviceIdType.MESH
        )

    span = max(last, 1)
    pl.semaphore_wait(barrier, 1 + (z + span - 1) // span + (last - z + span - 1) // span)

    @pl.when(z < last)
    def _():
        to_right(0, own_ref).start()

    @pl.when(z > 0)
    def _():
        to_left(0, own_ref).start()

    to_pair(z, own_ref).start()
    here = pltpu.make_async_copy(own_ref, block(z), local_sem)
    here.start()

    for s in range(last):

        @pl.when(z > s)
        def _():
            c = z - 1 - s
            copy(block(c), block(c), r_send.at[s], r_recv.at[s], left).wait_recv()
            if s + 1 < last:

                @pl.when(z < last)
                def _():
                    to_right(s + 1).start()

            to_pair(c).start()

        @pl.when(z < last - s)
        def _():
            c = z + 1 + s
            copy(block(c), block(c), l_send.at[s], l_recv.at[s], right).wait_recv()
            if s + 1 < last:

                @pl.when(z > 0)
                def _():
                    to_left(s + 1).start()

            to_pair(c).start()

    for s in range(last):

        @pl.when((z < last) & (z >= s))
        def _():
            to_right(s).wait_send()

        @pl.when((z > 0) & (last - z >= s))
        def _():
            to_left(s).wait_send()

    here.wait()
    for c in range(length):
        to_pair(c).wait_send()
        theirs = out_ref.at[pl.ds((2 * c + 1 - p) * rows, rows)]
        copy(theirs, theirs, y_send.at[c], y_recv.at[c], pair).wait_recv()


def gather_line(own, length):
    rows, cols = own.shape
    dma = pltpu.SemaphoreType.DMA
    steps = max(length - 1, 1)
    return pl.pallas_call(
        functools.partial(gather_kernel, length),
        out_shape=jax.ShapeDtypeStruct((2 * length * rows, cols), own.dtype),
        in_specs=[pl.BlockSpec(memory_space=pltpu.VMEM)],
        out_specs=pl.BlockSpec(memory_space=pl.ANY),
        scratch_shapes=[dma, dma((length,)), dma((length,))] + [dma((steps,))] * 4,
        compiler_params=pltpu.CompilerParams(collective_id=0, has_side_effects=True),
        name="gather_rows",
    )(own)


def body(activations, cotangent, weights, first_moment, second_moment, *, n, parts):
    f = lax.axis_index("fsdp")
    z, p = f // 2, f % 2
    length = n // 2
    depth, cols = weights.shape
    rows = depth // n
    tok, width = activations.shape
    pair = [(i, i ^ 1) for i in range(n)]

    packed = jnp.concatenate([weights, first_moment, second_moment], axis=1).astype(jnp.bfloat16)
    lines = [[2 * i + q for i in range(length)] for q in range(2)]
    packed = lax.optimization_barrier(packed.reshape(length, 2, rows, 3 * cols))
    along = lax.all_to_all(packed, "fsdp", 0, 0, axis_index_groups=lines)
    blocks = activations.reshape(tok, width // (2 * rows), 2, rows)
    keep = lax.dynamic_index_in_dim(blocks, p, 2, False).reshape(tok, width // 2)
    give = lax.dynamic_index_in_dim(blocks, 1 - p, 2, False).reshape(tok, width // 2)
    got = lax.ppermute(give, "fsdp", pair)
    cot_peer = lax.ppermute(cotangent, "fsdp", pair)
    mine = lax.all_gather(keep, "tensor")
    theirs = lax.all_gather(got, "tensor")

    def product(a, b):
        return lax.dot_general(a, b, (((0,), (0,)), ((), ())), preferred_element_type=jnp.float32)

    groups = length // parts

    def term(c):
        at = (c // groups, 0, (c % groups) * rows)
        near, far = (
            lax.dynamic_slice(array, at, (1, tok, rows))[0] for array in (mine, theirs)
        )
        total = product(near, cotangent) + product(far, cot_peer)
        return lax.optimization_barrier(total.astype(jnp.bfloat16))

    gradient = reduce_line(term, z, length)

    stay = lax.dynamic_index_in_dim(along, p, 1, False)
    across = lax.ppermute(lax.dynamic_index_in_dim(along, 1 - p, 1, False), "fsdp", pair)
    moved = jnp.where(p == 0, jnp.stack([stay, across], 1), jnp.stack([across, stay], 1))

    def owned(k):
        pieces = [moved[i // 2, i % 2, :, k * cols : (k + 1) * cols] for i in range(n)]
        return lax.optimization_barrier(jnp.concatenate(pieces, axis=1)).astype(jnp.float32)

    weights_new, first_new, second_new = adam_update(owned(0), owned(1), owned(2), gradient)
    rounded = weights_new.astype(jnp.bfloat16)
    weights_bf16 = gather_line(rounded, length)
    return (weights_new, first_new, second_new, weights_bf16)


CHUNKS = 2
LANE = 128


def fsdp_kernel(
    n, parts, chunks, act, cot, w_in, m_in, v_in, w_out, m_out, v_out, b_out,
    a_buf, at_buf, c_buf, st_in, st_out, fin, stg, up, dn, tmp, stage, wb,
    loc_sem, st_sem, out_sem, own_sem, give_s, give_r, cot_s, cot_r,
    t_send, t_recv, fin_s, fin_r, stg_s, stg_r, fwd_s, fwd_r,
    up_s, up_r, dn_s, dn_r, y_send, y_recv, r_send, r_recv, l_send, l_recv,
):
    f = lax.axis_index("fsdp")
    t = lax.axis_index("tensor")
    z, p = f // 2, f % 2
    length = n // 2
    last = length - 1
    rows, width = a_buf.shape[-1], act.shape[1]
    cols = w_in.shape[1]
    part = rows // chunks
    pair = f + 1 - 2 * p
    bits = [b for b in (1 << i for i in range(parts.bit_length()))][::-1]
    bits = [b for b in bits if b < parts]

    def copy(src, dst, send, recv, axis, target):
        return pltpu.make_async_remote_copy(
            src_ref=src, dst_ref=dst, send_sem=send, recv_sem=recv,
            device_id={axis: target}, device_id_type=pl.DeviceIdType.MESH,
        )

    def flip(b):
        return t + b - 2 * b * ((t // b) % 2)

    barrier = pltpu.get_barrier_semaphore()

    def greet(axis, target):
        pl.semaphore_signal(
            barrier, inc=1, device_id={axis: target}, device_id_type=pl.DeviceIdType.MESH
        )

    greet("fsdp", pair)
    for j in range(1, length):
        greet("fsdp", ((z + j) % length) * 2 + p)
    for b in bits:
        greet("tensor", flip(b))
    pl.semaphore_wait(barrier, length + len(bits))

    def feature(q):
        return act.at[:, pl.ds(pl.multiple_of(q * rows, rows), rows)]

    give = copy(feature(1 - p), a_buf.at[1, t], give_s, give_r, "fsdp", pair)
    give.start()
    cots = copy(cot, c_buf.at[1], cot_s, cot_r, "fsdp", pair)
    cots.start()
    mine = pltpu.make_async_copy(feature(p), a_buf.at[0, t], loc_sem.at[0])
    mine.start()
    here = pltpu.make_async_copy(cot, c_buf.at[0], loc_sem.at[1])
    here.start()

    def held(i):
        found = [t]
        for b in bits[:i]:
            found = found + [h + b - 2 * b * ((t // b) % 2) for h in found]
        return found

    def block_copy(which, i, h):
        return copy(
            a_buf.at[which, h], a_buf.at[which, h], t_send.at[which, i, h],
            t_recv.at[which, h], "tensor", flip(bits[i]),
        )

    def spread_own(which):
        for i in range(len(bits)):
            block_copy(which, i, t).start()

    def spread_round(which, i):
        b = bits[i]
        for h in held(i):
            g = h + b - 2 * b * ((t // b) % 2)
            block_copy(which, i, g).wait_recv()
            for j in range(i + 1, len(bits)):
                block_copy(which, j, g).start()

    def spread_done(which):
        for i in range(len(bits)):
            for h in held(i):
                block_copy(which, i, h).wait_send()

    mine.wait()
    spread_own(0)

    def load_state(i, slot):
        at = pl.ds(pl.multiple_of((i % n) * rows + (i // n) * part, part), part)
        return [
            pltpu.make_async_copy(src.at[at], st_in.at[slot, a], st_sem.at[slot, a])
            for a, src in enumerate((w_in, m_in, v_in))
        ]

    def span(k):
        return pl.ds(pl.multiple_of(k * part, part), part)

    def fin_copy(k, zs, zd):
        return copy(
            st_out.at[2 * zd + p, span(k)], fin.at[2 * zs + p, span(k)],
            fin_s.at[k, zd], fin_r.at[k, zs], "fsdp", 2 * zd + p,
        )

    def stg_copy(k, zs, zd):
        return copy(
            st_out.at[2 * zd + 1 - p, span(k)], stg.at[zs, span(k)],
            stg_s.at[k, zd], stg_r.at[k, zs], "fsdp", 2 * zd + p,
        )

    for c in load_state(0, 0):
        c.start()

    def pack(i, carry):
        slot = i % 2

        @pl.when(i + 1 < chunks * n)
        def _():
            for c in load_state(i + 1, (i + 1) % 2):
                c.start()

        for c in load_state(i, slot):
            c.wait()
        d, k = i % n, i // n
        for a in range(3):
            st_out[d, span(k), a * cols : (a + 1) * cols] = st_in[slot, a].astype(jnp.bfloat16)

        @pl.when(d == f)
        def _():
            fin[d, span(k), :] = st_out[d, span(k), :]

        zd = d // 2

        @pl.when((zd != z) & (d % 2 == p))
        def _():
            fin_copy(k, z, zd).start()

        @pl.when((zd != z) & (d % 2 != p))
        def _():
            stg_copy(k, z, zd).start()

        return carry

    lax.fori_loop(0, chunks * n, pack, 0)

    def turn(which):
        def tile(i, carry):
            j, r = i // (rows // LANE), i % (rows // LANE)
            at = pl.ds(pl.multiple_of(r * LANE, LANE), LANE)
            at_buf[which, j, at, :] = a_buf[which, j, :, at].T
            return carry

        lax.fori_loop(0, parts * (rows // LANE), tile, 0)

    give.wait_recv()
    spread_own(1)
    for i in range(len(bits)):
        spread_round(0, i)
    turn(0)
    for i in range(len(bits)):
        spread_round(1, i)
    turn(1)

    def forward(k, zs):
        src = stg.at[zs, span(k)]
        return copy(
            src, fin.at[2 * zs + p, span(k)], fwd_s.at[k, zs], fwd_r.at[k, zs], "fsdp", pair
        )

    def forward_own(k):
        return copy(
            st_out.at[pair, span(k)], fin.at[f, span(k)],
            fwd_s.at[k, z], fwd_r.at[k, z], "fsdp", pair,
        )

    here.wait()
    cots.wait()

    def forward_state(k):
        forward_own(k).start()
        for j in range(1, length):
            zs = (z + j) % length
            stg_copy(k, zs, z).wait_recv()
            forward(k, zs).start()

    def state_here(k):
        for j in range(1, length):
            fin_copy(k, (z + j) % length, z).wait_recv()
        for zs in range(length):
            copy(
                stg.at[zs, span(k)], fin.at[2 * zs + 1 - p, span(k)],
                fwd_s.at[k, zs], fwd_r.at[k, zs], "fsdp", pair,
            ).wait_recv()

    block_n = 2 * LANE

    def term(d, k):
        def tile(i, carry):
            at = pl.ds(pl.multiple_of(i * block_n, block_n), block_n)
            total = jnp.dot(
                at_buf[0, d, span(k), :], c_buf[0, :, at], preferred_element_type=jnp.float32
            ) + jnp.dot(
                at_buf[1, d, span(k), :], c_buf[1, :, at], preferred_element_type=jnp.float32
            )
            tmp[:, at] = total
            return carry

        lax.fori_loop(0, width // block_n, tile, 0)

    def send_up(k, s):
        slot = s - jnp.minimum(z, 1)
        return copy(up.at[k, slot], up.at[k, s], up_s.at[k, s], up_r.at[k, s], "fsdp", f + 2)

    def send_dn(k, s):
        slot = s - jnp.minimum(last - z, 1)
        return copy(dn.at[k, slot], dn.at[k, s], dn_s.at[k, s], dn_r.at[k, s], "fsdp", f - 2)

    def take_up(k, s):
        copy(up.at[k, s], up.at[k, s], up_s.at[k, s], up_r.at[k, s], "fsdp", f - 2).wait_recv()

    def take_dn(k, s):
        copy(dn.at[k, s], dn.at[k, s], dn_s.at[k, s], dn_r.at[k, s], "fsdp", f + 2).wait_recv()

    def add_in(ref, k, slot, first):
        @pl.when(first)
        def _():
            ref[k, slot] = tmp[...].astype(jnp.bfloat16)

        @pl.when(jnp.logical_not(first))
        def _():
            ref[k, slot] = (tmp[...] + ref[k, slot].astype(jnp.float32)).astype(jnp.bfloat16)

    def reduce_step(k, s):
        @pl.when(z <= s)
        def _():
            term(last + z - s, k)
            if s:

                @pl.when(z > 0)
                def _():
                    take_up(k, s - 1)

            add_in(up, k, s - jnp.minimum(z, 1), z == 0)
            send_up(k, s).start()

        @pl.when(z >= last - s)
        def _():
            term(s - last + z, k)
            if s:

                @pl.when(z < last)
                def _():
                    take_dn(k, s - 1)

            add_in(dn, k, s - jnp.minimum(last - z, 1), z == last)
            send_dn(k, s).start()

    sub = stage.shape[2]
    subs = part // sub

    def out_copies(i, slot):
        at = pl.ds(pl.multiple_of(i * sub, sub), sub)
        return [
            pltpu.make_async_copy(stage.at[slot, a], dst.at[at], out_sem.at[slot, a])
            for a, dst in enumerate((w_out, m_out, v_out))
        ]

    def adam(k):
        term(z, k)

        @pl.when(z > 0)
        def _():
            take_up(k, last - 1)
            tmp[...] += up[k, last - 1].astype(jnp.float32)

        @pl.when(z < last)
        def _():
            take_dn(k, last - 1)
            tmp[...] += dn[k, last - 1].astype(jnp.float32)

        state_here(k)

        def piece(j, carry):
            i = k * subs + j
            slot = i % 2

            @pl.when(i >= 2)
            def _():
                for c in out_copies(i - 2, slot):
                    c.wait()

            at = pl.ds(pl.multiple_of(i * sub, sub), sub)
            loc = pl.ds(pl.multiple_of(j * sub, sub), sub)
            state = [fin[src, at, :].astype(jnp.float32) for src in range(n)]
            old = [
                jnp.concatenate([x[:, a * cols : (a + 1) * cols] for x in state], axis=1)
                for a in range(3)
            ]
            new = adam_update(*old, tmp[loc, :])
            for a in range(3):
                stage[slot, a] = new[a]
            wb[k, loc, :] = new[0].astype(jnp.bfloat16)
            for c in out_copies(i, slot):
                c.start()
            return carry

        lax.fori_loop(0, subs, piece, 0)

    def block(c, q, k):
        return b_out.at[pl.ds(pl.multiple_of((2 * c + q) * rows + k * part, part), part)]

    def to_pair(k, c, src=None):
        src = block(c, p, k) if src is None else src
        return copy(src, block(c, p, k), y_send.at[k, c], y_recv.at[k, c], "fsdp", pair)

    def to_right(k, s, src=None):
        src = block(z - s, p, k) if src is None else src
        return copy(
            src, block(z - s, p, k), r_send.at[k, s], r_recv.at[k, s], "fsdp", f + 2
        )

    def to_left(k, s, src=None):
        src = block(z + s, p, k) if src is None else src
        return copy(
            src, block(z + s, p, k), l_send.at[k, s], l_recv.at[k, s], "fsdp", f - 2
        )

    def keep(k):
        return pltpu.make_async_copy(wb.at[k], block(z, p, k), own_sem.at[k])

    def gather_start(k):
        to_pair(k, z, wb.at[k]).start()

        @pl.when(z < last)
        def _():
            to_right(k, 0, wb.at[k]).start()

        @pl.when(z > 0)
        def _():
            to_left(k, 0, wb.at[k]).start()

        keep(k).start()

    def gather_step(k, s):
        @pl.when(z > s)
        def _():
            c = z - 1 - s
            got = block(c, p, k)
            copy(got, got, r_send.at[k, s], r_recv.at[k, s], "fsdp", f - 2).wait_recv()
            if s + 1 < last:

                @pl.when(z < last)
                def _():
                    to_right(k, s + 1).start()

            to_pair(k, c).start()

        @pl.when(z < last - s)
        def _():
            c = z + 1 + s
            got = block(c, p, k)
            copy(got, got, l_send.at[k, s], l_recv.at[k, s], "fsdp", f + 2).wait_recv()
            if s + 1 < last:

                @pl.when(z > 0)
                def _():
                    to_left(k, s + 1).start()

            to_pair(k, c).start()

    forward_state(0)
    for s in range(last):
        reduce_step(0, s)
    for k in range(1, chunks):
        forward_state(k)
        reduce_step(k, 0)
        adam(k - 1)
        gather_start(k - 1)
        for s in range(1, last):
            reduce_step(k, s)
            gather_step(k - 1, s - 1)
        if last > 1:
            gather_step(k - 1, last - 1)
    adam(chunks - 1)
    gather_start(chunks - 1)
    for s in range(last):
        gather_step(chunks - 1, s)

    give.wait_send()
    spread_done(0)
    spread_done(1)
    for j in (2, 1):
        for c in out_copies(chunks * subs - j, (chunks * subs - j) % 2):
            c.wait()
    for k in range(chunks):
        keep(k).wait()
        for j in range(1, length):
            zd = (z + j) % length
            fin_copy(k, z, zd).wait_send()
            stg_copy(k, z, zd).wait_send()
        for zs in range(length):
            forward(k, zs).wait_send()
        for s in range(last):

            @pl.when(z <= s)
            def _():
                send_up(k, s).wait_send()

            @pl.when(z >= last - s)
            def _():
                send_dn(k, s).wait_send()

            @pl.when((z < last) & (z >= s))
            def _():
                to_right(k, s).wait_send()

            @pl.when((z > 0) & (last - z >= s))
            def _():
                to_left(k, s).wait_send()

        for c in range(length):
            to_pair(k, c).wait_send()
            theirs = block(c, 1 - p, k)
            copy(theirs, theirs, y_send.at[k, c], y_recv.at[k, c], "fsdp", pair).wait_recv()


def fast_body(activations, cotangent, weights, first_moment, second_moment, *, n, parts):
    depth, cols = weights.shape
    tok, width = activations.shape
    rows = depth // n
    length, chunks = n // 2, CHUNKS
    part = rows // chunks
    sub = part // 4
    rounds = parts.bit_length() - 1
    dma = pltpu.SemaphoreType.DMA
    half, full = jnp.bfloat16, jnp.float32
    hops = max(length - 1, 1)
    row = jax.ShapeDtypeStruct((rows, width), full)
    anywhere = pl.BlockSpec(memory_space=pl.ANY)
    return tuple(
        pl.pallas_call(
            functools.partial(fsdp_kernel, n, parts, chunks),
            out_shape=(row, row, row, jax.ShapeDtypeStruct((depth, width), half)),
            in_specs=[anywhere] * 5,
            out_specs=(anywhere,) * 4,
            scratch_shapes=[
                pltpu.VMEM((2, parts, tok, rows), half),
                pltpu.VMEM((2, parts, rows, tok), half),
                pltpu.VMEM((2, tok, width), half),
                pltpu.VMEM((2, 3, part, cols), full),
                pltpu.VMEM((n, rows, 3 * cols), half),
                pltpu.VMEM((n, rows, 3 * cols), half),
                pltpu.VMEM((length, rows, 3 * cols), half),
                pltpu.VMEM((chunks, hops, part, width), half),
                pltpu.VMEM((chunks, hops, part, width), half),
                pltpu.VMEM((part, width), full),
                pltpu.VMEM((2, 3, sub, width), full),
                pltpu.VMEM((chunks, part, width), half),
                dma((2,)), dma((2, 3)), dma((2, 3)), dma((chunks,)),
                dma, dma, dma, dma,
                dma((2, rounds, parts)), dma((2, parts)),
            ]
            + [dma((chunks, length))] * 6
            + [dma((chunks, hops))] * 4
            + [dma((chunks, length))] * 2
            + [dma((chunks, hops))] * 4,
            compiler_params=pltpu.CompilerParams(
                collective_id=0, has_side_effects=True, vmem_limit_bytes=67043328
            ),
            name="fsdp_step",
        )(activations, cotangent, weights, first_moment, second_moment)
    )


def solution(mesh):
    n, parts = mesh.shape["fsdp"], mesh.shape["tensor"]

    def run(*arrays):
        rows, width = arrays[2].shape[0] // n, arrays[0].shape[1]
        fits = rows % LANE == 0 and rows % (64 * CHUNKS) == 0 and n == 2 * parts
        if fits and width == 2 * rows and parts & (parts - 1) == 0:
            return fast_body(*arrays, n=n, parts=parts)
        return body(*arrays, n=n, parts=parts)

    return jax.shard_map(
        run,
        mesh=mesh,
        in_specs=(
            P("fsdp", "tensor"),
            P("fsdp", "tensor"),
            P(None, ("tensor", "fsdp")),
            P(None, ("tensor", "fsdp")),
            P(None, ("tensor", "fsdp")),
        ),
        out_specs=(
            P("fsdp", "tensor"),
            P("fsdp", "tensor"),
            P("fsdp", "tensor"),
            P(None, "tensor"),
        ),
        check_vma=False,
    )
```

profile of v0, /device:TPU:0, one launch (start us, length us, event | category | flops | bytes accessed | tf_op | source)
XLA Modules:
  0.0 361.5 jit_solution(10703951653125208893)
XLA Ops:
  0.6 0.0 copy-start.1
  0.6 5.6 %copy.9.w_in = f32[5120,160]{1,0:T(8,128)} copy(f32[5120,160]{0,1:T(8,128)} %param.7) | data formatting | bytes 6553600 | tf_op args[2]
  6.2 0.0 copy-done.1
  6.2 3.7 %copy.10.m_in = f32[5120,160]{1,0:T(8,128)} copy(f32[5120,160]{0,1:T(8,128)S(1)} %copy-done.1) | data formatting | bytes 6553600 | tf_op args[3]
  9.9 5.5 %copy.11.v_in = f32[5120,160]{1,0:T(8,128)} copy(f32[5120,160]{0,1:T(8,128)} %param.9) | data formatting | bytes 6553600 | tf_op args[4]
  15.4 328.7 %fsdp_step.1 = (f32[640,1280]{1,0:T(8,128)}, f32[640,1280]{1,0:T(8,128)}, f32[640,1280]{1,0:T(8,128)}, bf16[5120,1280]{1,0:T(8,128)(2,1)}) custom-call(bf16[1024,1280]{1,0:T(8,128)(2,1)} %act.1, bf16[1024,1280]{1,0:T(8,128)(2,1)} %cot.1, f32[5120,160]{1,0:T(8,128)} %copy.9.w_in, f32[5120,160]{1,0:T(8,128)} %copy.10.m_in, f32[5120,160]{1,0:T(8,128)} %copy.11.v_in), custom_call_target="tpu_custom_call" | custom-call | tf_op jit(solution)/shard_map/fsdp_step/pallas_call | solution.py:672
  344.1 0.0 copy-start
  344.1 4.0 %copy.16 = f32[640,1280]{1,0:T(8,128)} copy(f32[640,1280]{1,0:T(8,128)} %get-tuple-element.8) | data formatting | bytes 6553600
  348.1 4.6 %copy.17 = f32[640,1280]{1,0:T(8,128)} copy(f32[640,1280]{1,0:T(8,128)} %get-tuple-element.9) | data formatting | bytes 6553600
  352.7 3.8 %copy.18 = f32[640,1280]{1,0:T(8,128)} copy(f32[640,1280]{1,0:T(8,128)} %get-tuple-element.10) | data formatting | bytes 6553600
  356.6 0.0 copy-done
  356.6 4.9 %copy.19 = bf16[5120,1280]{1,0:T(8,128)(2,1)} copy(bf16[5120,1280]{1,0:T(8,128)(2,1)S(1)} %copy-done) | data formatting | bytes 26214400
Async XLA Ops:
  0.6 5.6 %copy-start.1 = (f32[5120,160]{0,1:T(8,128)S(1)}, f32[5120,160]{0,1:T(8,128)}, u32[]{:S(2)}) copy-start(f32[5120,160]{0,1:T(8,128)} %param.8) | copy-start | bytes 9830404
  344.1 12.4 %copy-start = (bf16[5120,1280]{1,0:T(8,128)(2,1)S(1)}, bf16[5120,1280]{1,0:T(8,128)(2,1)}, u32[]{:S(2)}) copy-start(bf16[5120,1280]{1,0:T(8,128)(2,1)} %get-tuple-element.11) | copy-start | bytes 39321604
where the time goes:
time: 362 us
  Pallas kernels  329 us (91%)
  local copies, waits for them, and re-layouts  32.2 us (9%)
    pallas_call x1, Pallas kernels, fast_body(): pl.pallas_call(functools.partial(fsdp_kernel, n, parts, chunks), out_shap...  329 us
    unnamed x11, local copies, waits for them, and re-layouts  32.2 us

commit v1 on v0

--- a/solution.py
+++ b/solution.py
@@ -227,14 +227,13 @@
     return (weights_new, first_new, second_new, weights_bf16)
 
 
-CHUNKS = 2
 LANE = 128
 
 
 def fsdp_kernel(
-    n, parts, chunks, act, cot, w_in, m_in, v_in, w_out, m_out, v_out, b_out,
-    a_buf, at_buf, c_buf, st_in, st_out, fin, stg, up, dn, tmp, stage, wb,
-    loc_sem, st_sem, out_sem, own_sem, give_s, give_r, cot_s, cot_r,
+    n, parts, sizes, act, cot, w_in, m_in, v_in, w_out, m_out, v_out, b_out,
+    raw, give_t, at_buf, c_buf, st_in, st_out, fin, stg, up, dn, tmp, old, stage, wb,
+    raw_sem, loc_sem, st_sem, out_sem, own_sem, give_s, give_r, cot_s, cot_r,
     t_send, t_recv, fin_s, fin_r, stg_s, stg_r, fwd_s, fwd_r,
     up_s, up_r, dn_s, dn_r, y_send, y_recv, r_send, r_recv, l_send, l_recv,
 ):
@@ -243,12 +242,11 @@
     z, p = f // 2, f % 2
     length = n // 2
     last = length - 1
-    rows, width = a_buf.shape[-1], act.shape[1]
-    cols = w_in.shape[1]
-    part = rows // chunks
+    tok, width = act.shape
+    rows, cols = at_buf.shape[2], w_in.shape[0]
     pair = f + 1 - 2 * p
-    bits = [b for b in (1 << i for i in range(parts.bit_length()))][::-1]
-    bits = [b for b in bits if b < parts]
+    bits = [1 << i for i in range(parts.bit_length() - 1)][::-1]
+    starts = [sum(sizes[:k]) for k in range(len(sizes))]
 
     def copy(src, dst, send, recv, axis, target):
         return pltpu.make_async_remote_copy(
@@ -256,8 +254,41 @@
             device_id={axis: target}, device_id_type=pl.DeviceIdType.MESH,
         )
 
-    def flip(b):
-        return t + b - 2 * b * ((t // b) % 2)
+    def crossed(i, b):
+        return i + b - 2 * b * ((t // b) % 2)
+
+    def ring(j):
+        return (z + j) % length
+
+    def span(k):
+        return pl.ds(starts[k], sizes[k])
+
+    def lanes(i, size):
+        return pl.ds(pl.multiple_of(i * size, size), size)
+
+    def feature(q):
+        return lanes(q, rows)
+
+    raw_copies = [
+        pltpu.make_async_copy(act.at[:, feature(q)], raw.at[i], raw_sem.at[i])
+        for i, q in enumerate((1 - p, p))
+    ]
+    for c in raw_copies:
+        c.start()
+    here = pltpu.make_async_copy(cot, c_buf.at[0], loc_sem)
+    here.start()
+
+    def load_state(u, slot):
+        d = 2 * ring(u + 1) + (p + 1 + u // length) % 2
+        return [
+            pltpu.make_async_copy(
+                src.at[:, lanes(d, rows)], st_in.at[slot, a], st_sem.at[slot, a]
+            )
+            for a, src in enumerate((w_in, m_in, v_in))
+        ]
+
+    for c in load_state(0, 0):
+        c.start()
 
     barrier = pltpu.get_barrier_semaphore()
 
@@ -268,43 +299,43 @@
 
     greet("fsdp", pair)
     for j in range(1, length):
-        greet("fsdp", ((z + j) % length) * 2 + p)
+        greet("fsdp", 2 * ring(j) + p)
     for b in bits:
-        greet("tensor", flip(b))
+        greet("tensor", crossed(t, b))
     pl.semaphore_wait(barrier, length + len(bits))
 
-    def feature(q):
-        return act.at[:, pl.ds(pl.multiple_of(q * rows, rows), rows)]
-
-    give = copy(feature(1 - p), a_buf.at[1, t], give_s, give_r, "fsdp", pair)
-    give.start()
-    cots = copy(cot, c_buf.at[1], cot_s, cot_r, "fsdp", pair)
-    cots.start()
-    mine = pltpu.make_async_copy(feature(p), a_buf.at[0, t], loc_sem.at[0])
-    mine.start()
-    here = pltpu.make_async_copy(cot, c_buf.at[0], loc_sem.at[1])
-    here.start()
+    head = tok // 4
+
+    def cot_copy(i):
+        at = pl.ds(0, head) if i == 0 else pl.ds(head, tok - head)
+        return copy(cot.at[at], c_buf.at[1, at], cot_s.at[i], cot_r.at[i], "fsdp", pair)
+
+    def turn(src, dst):
+        def tile(r, carry):
+            dst[lanes(r, LANE), :] = src[:, lanes(r, LANE)].T
+            return carry
+
+        lax.fori_loop(0, rows // LANE, tile, 0)
+
+    def block_copy(which, i, h):
+        return copy(
+            at_buf.at[which, h], at_buf.at[which, h], t_send.at[which, i, h],
+            t_recv.at[which, h], "tensor", crossed(t, bits[i]),
+        )
 
     def held(i):
         found = [t]
         for b in bits[:i]:
-            found = found + [h + b - 2 * b * ((t // b) % 2) for h in found]
+            found = found + [crossed(h, b) for h in found]
         return found
-
-    def block_copy(which, i, h):
-        return copy(
-            a_buf.at[which, h], a_buf.at[which, h], t_send.at[which, i, h],
-            t_recv.at[which, h], "tensor", flip(bits[i]),
-        )
 
     def spread_own(which):
         for i in range(len(bits)):
             block_copy(which, i, t).start()
 
     def spread_round(which, i):
-        b = bits[i]
         for h in held(i):
-            g = h + b - 2 * b * ((t // b) % 2)
+            g = crossed(h, bits[i])
             block_copy(which, i, g).wait_recv()
             for j in range(i + 1, len(bits)):
                 block_copy(which, j, g).start()
@@ -314,152 +345,130 @@
             for h in held(i):
                 block_copy(which, i, h).wait_send()
 
-    mine.wait()
+    cot_copy(0).start()
+    raw_copies[0].wait()
+    turn(raw.at[0], give_t)
+    give = copy(give_t, at_buf.at[1, t], give_s, give_r, "fsdp", pair)
+    give.start()
+    cot_copy(1).start()
+    raw_copies[1].wait()
+    turn(raw.at[1], at_buf.at[0, t])
     spread_own(0)
 
-    def load_state(i, slot):
-        at = pl.ds(pl.multiple_of((i % n) * rows + (i // n) * part, part), part)
-        return [
-            pltpu.make_async_copy(src.at[at], st_in.at[slot, a], st_sem.at[slot, a])
-            for a, src in enumerate((w_in, m_in, v_in))
-        ]
-
-    def span(k):
-        return pl.ds(pl.multiple_of(k * part, part), part)
-
-    def fin_copy(k, zs, zd):
+    def fin_copy(zs, zd):
         return copy(
-            st_out.at[2 * zd + p, span(k)], fin.at[2 * zs + p, span(k)],
-            fin_s.at[k, zd], fin_r.at[k, zs], "fsdp", 2 * zd + p,
-        )
-
-    def stg_copy(k, zs, zd):
+            st_out.at[2 * zd + p], fin.at[2 * zs + p], fin_s.at[zd], fin_r.at[zs],
+            "fsdp", 2 * zd + p,
+        )
+
+    def stg_copy(zs, zd):
         return copy(
-            st_out.at[2 * zd + 1 - p, span(k)], stg.at[zs, span(k)],
-            stg_s.at[k, zd], stg_r.at[k, zs], "fsdp", 2 * zd + p,
-        )
-
-    for c in load_state(0, 0):
-        c.start()
-
-    def pack(i, carry):
-        slot = i % 2
-
-        @pl.when(i + 1 < chunks * n)
-        def _():
-            for c in load_state(i + 1, (i + 1) % 2):
+            st_out.at[2 * zd + 1 - p], stg.at[zs], stg_s.at[zd], stg_r.at[zs],
+            "fsdp", 2 * zd + p,
+        )
+
+    def pack(u, carry):
+        slot = u % 2
+
+        @pl.when(u + 1 < n)
+        def _():
+            for c in load_state(u + 1, (u + 1) % 2):
                 c.start()
 
-        for c in load_state(i, slot):
+        for c in load_state(u, slot):
             c.wait()
-        d, k = i % n, i // n
+        zd, q = ring(u + 1), (p + 1 + u // length) % 2
+        d = 2 * zd + q
         for a in range(3):
-            st_out[d, span(k), a * cols : (a + 1) * cols] = st_in[slot, a].astype(jnp.bfloat16)
+            st_out[d, a * cols : (a + 1) * cols, :] = st_in[slot, a].astype(jnp.bfloat16)
 
         @pl.when(d == f)
         def _():
-            fin[d, span(k), :] = st_out[d, span(k), :]
-
-        zd = d // 2
-
-        @pl.when((zd != z) & (d % 2 == p))
-        def _():
-            fin_copy(k, z, zd).start()
-
-        @pl.when((zd != z) & (d % 2 != p))
-        def _():
-            stg_copy(k, z, zd).start()
+            fin[d] = st_out[d]
+
+        @pl.when((zd != z) & (q == p))
+        def _():
+            fin_copy(z, zd).start()
+
+        @pl.when((zd != z) & (q != p))
+        def _():
+            stg_copy(z, zd).start()
 
         return carry
 
-    lax.fori_loop(0, chunks * n, pack, 0)
-
-    def turn(which):
-        def tile(i, carry):
-            j, r = i // (rows // LANE), i % (rows // LANE)
-            at = pl.ds(pl.multiple_of(r * LANE, LANE), LANE)
-            at_buf[which, j, at, :] = a_buf[which, j, :, at].T
-            return carry
-
-        lax.fori_loop(0, parts * (rows // LANE), tile, 0)
-
+    lax.fori_loop(0, n, pack, 0)
+
+    for i in range(len(bits)):
+        spread_round(0, i)
     give.wait_recv()
     spread_own(1)
     for i in range(len(bits)):
-        spread_round(0, i)
-    turn(0)
-    for i in range(len(bits)):
         spread_round(1, i)
-    turn(1)
-
-    def forward(k, zs):
-        src = stg.at[zs, span(k)]
-        return copy(
-            src, fin.at[2 * zs + p, span(k)], fwd_s.at[k, zs], fwd_r.at[k, zs], "fsdp", pair
-        )
-
-    def forward_own(k):
-        return copy(
-            st_out.at[pair, span(k)], fin.at[f, span(k)],
-            fwd_s.at[k, z], fwd_r.at[k, z], "fsdp", pair,
-        )
-
     here.wait()
-    cots.wait()
-
-    def forward_state(k):
-        forward_own(k).start()
+    for i in range(2):
+        cot_copy(i).wait_recv()
+
+    def forward(zs, src=None):
+        src = stg.at[zs] if src is None else src
+        return copy(src, fin.at[2 * zs + p], fwd_s.at[zs], fwd_r.at[zs], "fsdp", pair)
+
+    def forward_state(j):
+        zs = ring(length - j)
+        stg_copy(zs, z).wait_recv()
+        forward(zs).start()
+
+    def state_here():
         for j in range(1, length):
-            zs = (z + j) % length
-            stg_copy(k, zs, z).wait_recv()
-            forward(k, zs).start()
-
-    def state_here(k):
-        for j in range(1, length):
-            fin_copy(k, (z + j) % length, z).wait_recv()
+            fin_copy(ring(j), z).wait_recv()
         for zs in range(length):
-            copy(
-                stg.at[zs, span(k)], fin.at[2 * zs + 1 - p, span(k)],
-                fwd_s.at[k, zs], fwd_r.at[k, zs], "fsdp", pair,
-            ).wait_recv()
-
-    block_n = 2 * LANE
+            got = fin.at[2 * zs + 1 - p]
+            copy(stg.at[zs], got, fwd_s.at[zs], fwd_r.at[zs], "fsdp", pair).wait_recv()
 
     def term(d, k):
         def tile(i, carry):
-            at = pl.ds(pl.multiple_of(i * block_n, block_n), block_n)
-            total = jnp.dot(
-                at_buf[0, d, span(k), :], c_buf[0, :, at], preferred_element_type=jnp.float32
-            ) + jnp.dot(
-                at_buf[1, d, span(k), :], c_buf[1, :, at], preferred_element_type=jnp.float32
+            at = lanes(i, 2 * LANE)
+            tmp[: sizes[k], at] = sum(
+                jnp.dot(
+                    at_buf[b, d, span(k), :], c_buf[b, :, at],
+                    preferred_element_type=jnp.float32,
+                )
+                for b in range(2)
             )
-            tmp[:, at] = total
             return carry
 
-        lax.fori_loop(0, width // block_n, tile, 0)
+        lax.fori_loop(0, width // (2 * LANE), tile, 0)
 
     def send_up(k, s):
         slot = s - jnp.minimum(z, 1)
-        return copy(up.at[k, slot], up.at[k, s], up_s.at[k, s], up_r.at[k, s], "fsdp", f + 2)
+        return copy(
+            up.at[slot, span(k)], up.at[s, span(k)], up_s.at[k, s], up_r.at[k, s], "fsdp", f + 2
+        )
 
     def send_dn(k, s):
         slot = s - jnp.minimum(last - z, 1)
-        return copy(dn.at[k, slot], dn.at[k, s], dn_s.at[k, s], dn_r.at[k, s], "fsdp", f - 2)
+        return copy(
+            dn.at[slot, span(k)], dn.at[s, span(k)], dn_s.at[k, s], dn_r.at[k, s], "fsdp", f - 2
+        )
 
     def take_up(k, s):
-        copy(up.at[k, s], up.at[k, s], up_s.at[k, s], up_r.at[k, s], "fsdp", f - 2).wait_recv()
+        got = up.at[s, span(k)]
+        copy(got, got, up_s.at[k, s], up_r.at[k, s], "fsdp", f - 2).wait_recv()
 
     def take_dn(k, s):
-        copy(dn.at[k, s], dn.at[k, s], dn_s.at[k, s], dn_r.at[k, s], "fsdp", f + 2).wait_recv()
+        got = dn.at[s, span(k)]
+        copy(got, got, dn_s.at[k, s], dn_r.at[k, s], "fsdp", f + 2).wait_recv()
 
     def add_in(ref, k, slot, first):
+        mine = pl.ds(0, sizes[k])
+
         @pl.when(first)
         def _():
-            ref[k, slot] = tmp[...].astype(jnp.bfloat16)
+            ref[slot, span(k), :] = tmp[mine, :].astype(jnp.bfloat16)
 
         @pl.when(jnp.logical_not(first))
         def _():
-            ref[k, slot] = (tmp[...] + ref[k, slot].astype(jnp.float32)).astype(jnp.bfloat16)
+            total = tmp[mine, :] + ref[slot, span(k), :].astype(jnp.float32)
+            ref[slot, span(k), :] = total.astype(jnp.bfloat16)
 
     def reduce_step(k, s):
         @pl.when(z <= s)
@@ -487,32 +496,40 @@
             send_dn(k, s).start()
 
     sub = stage.shape[2]
-    subs = part // sub
 
     def out_copies(i, slot):
-        at = pl.ds(pl.multiple_of(i * sub, sub), sub)
         return [
-            pltpu.make_async_copy(stage.at[slot, a], dst.at[at], out_sem.at[slot, a])
+            pltpu.make_async_copy(stage.at[slot, a], dst.at[lanes(i, sub)], out_sem.at[slot, a])
             for a, dst in enumerate((w_out, m_out, v_out))
         ]
 
     def adam(k):
         term(z, k)
+        if k == 0:
+            state_here()
+
+        def spin(i, carry):
+            at = pl.ds(pl.multiple_of(starts[k] + i * LANE, LANE), LANE)
+            for a in range(3):
+                parts_of = [fin[src, a * cols : (a + 1) * cols, at] for src in range(n)]
+                old[a, lanes(i, LANE), :] = jnp.concatenate(parts_of, axis=0).T
+            return carry
+
+        lax.fori_loop(0, sizes[k] // LANE, spin, 0)
+        mine = pl.ds(0, sizes[k])
 
         @pl.when(z > 0)
         def _():
             take_up(k, last - 1)
-            tmp[...] += up[k, last - 1].astype(jnp.float32)
+            tmp[mine, :] += up[last - 1, span(k), :].astype(jnp.float32)
 
         @pl.when(z < last)
         def _():
             take_dn(k, last - 1)
-            tmp[...] += dn[k, last - 1].astype(jnp.float32)
-
-        state_here(k)
+            tmp[mine, :] += dn[last - 1, span(k), :].astype(jnp.float32)
 
         def piece(j, carry):
-            i = k * subs + j
+            i = starts[k] // sub + j
             slot = i % 2
 
             @pl.when(i >= 2)
@@ -520,25 +537,20 @@
                 for c in out_copies(i - 2, slot):
                     c.wait()
 
-            at = pl.ds(pl.multiple_of(i * sub, sub), sub)
-            loc = pl.ds(pl.multiple_of(j * sub, sub), sub)
-            state = [fin[src, at, :].astype(jnp.float32) for src in range(n)]
-            old = [
-                jnp.concatenate([x[:, a * cols : (a + 1) * cols] for x in state], axis=1)
-                for a in range(3)
-            ]
-            new = adam_update(*old, tmp[loc, :])
+            at = lanes(j, sub)
+            held_now = [old[a, at, :].astype(jnp.float32) for a in range(3)]
+            new = adam_update(*held_now, tmp[at, :])
             for a in range(3):
                 stage[slot, a] = new[a]
-            wb[k, loc, :] = new[0].astype(jnp.bfloat16)
+            wb[lanes(i, sub), :] = new[0].astype(jnp.bfloat16)
             for c in out_copies(i, slot):
                 c.start()
             return carry
 
-        lax.fori_loop(0, subs, piece, 0)
+        lax.fori_loop(0, sizes[k] // sub, piece, 0)
 
     def block(c, q, k):
-        return b_out.at[pl.ds(pl.multiple_of((2 * c + q) * rows + k * part, part), part)]
+        return b_out.at[pl.ds(pl.multiple_of((2 * c + q) * rows + starts[k], LANE), sizes[k])]
 
     def to_pair(k, c, src=None):
         src = block(c, p, k) if src is None else src
@@ -546,29 +558,26 @@
 
     def to_right(k, s, src=None):
         src = block(z - s, p, k) if src is None else src
-        return copy(
-            src, block(z - s, p, k), r_send.at[k, s], r_recv.at[k, s], "fsdp", f + 2
-        )
+        return copy(src, block(z - s, p, k), r_send.at[k, s], r_recv.at[k, s], "fsdp", f + 2)
 
     def to_left(k, s, src=None):
         src = block(z + s, p, k) if src is None else src
-        return copy(
-            src, block(z + s, p, k), l_send.at[k, s], l_recv.at[k, s], "fsdp", f - 2
-        )
+        return copy(src, block(z + s, p, k), l_send.at[k, s], l_recv.at[k, s], "fsdp", f - 2)
 
     def keep(k):
-        return pltpu.make_async_copy(wb.at[k], block(z, p, k), own_sem.at[k])
+        return pltpu.make_async_copy(wb.at[span(k)], block(z, p, k), own_sem.at[k])
 
     def gather_start(k):
-        to_pair(k, z, wb.at[k]).start()
+        mine = wb.at[span(k)]
+        to_pair(k, z, mine).start()
 
         @pl.when(z < last)
         def _():
-            to_right(k, 0, wb.at[k]).start()
+            to_right(k, 0, mine).start()
 
         @pl.when(z > 0)
         def _():
-            to_left(k, 0, wb.at[k]).start()
+            to_left(k, 0, mine).start()
 
         keep(k).start()
 
@@ -599,38 +608,41 @@
 
             to_pair(k, c).start()
 
-    forward_state(0)
+    forward(z, st_out.at[pair]).start()
+    waiting = []
     for s in range(last):
         reduce_step(0, s)
-    for k in range(1, chunks):
-        forward_state(k)
+        forward_state(s + 1)
+    for k in range(1, len(sizes)):
         reduce_step(k, 0)
         adam(k - 1)
         gather_start(k - 1)
+        for g in waiting:
+            gather_step(*g)
+        waiting = [(k - 1, s) for s in range(last)]
         for s in range(1, last):
             reduce_step(k, s)
-            gather_step(k - 1, s - 1)
-        if last > 1:
-            gather_step(k - 1, last - 1)
-    adam(chunks - 1)
-    gather_start(chunks - 1)
-    for s in range(last):
-        gather_step(chunks - 1, s)
+            gather_step(*waiting.pop(0))
+    adam(len(sizes) - 1)
+    gather_start(len(sizes) - 1)
+    for g in waiting + [(len(sizes) - 1, s) for s in range(last)]:
+        gather_step(*g)
 
     give.wait_send()
-    spread_done(0)
-    spread_done(1)
+    for i in range(2):
+        cot_copy(i).wait_send()
+        spread_done(i)
+    pieces = rows // sub
     for j in (2, 1):
-        for c in out_copies(chunks * subs - j, (chunks * subs - j) % 2):
+        for c in out_copies(pieces - j, (pieces - j) % 2):
             c.wait()
-    for k in range(chunks):
+    for j in range(1, length):
+        fin_copy(z, ring(j)).wait_send()
+        stg_copy(z, ring(j)).wait_send()
+    for zs in range(length):
+        forward(zs).wait_send()
+    for k in range(len(sizes)):
         keep(k).wait()
-        for j in range(1, length):
-            zd = (z + j) % length
-            fin_copy(k, z, zd).wait_send()
-            stg_copy(k, z, zd).wait_send()
-        for zs in range(length):
-            forward(k, zs).wait_send()
         for s in range(last):
 
             @pl.when(z <= s)
@@ -655,13 +667,20 @@
             copy(theirs, theirs, y_send.at[k, c], y_recv.at[k, c], "fsdp", pair).wait_recv()
 
 
+def row_chunks(rows):
+    tiles = rows // LANE
+    counts = [2] * (tiles // 2) + [1] * (tiles % 2)
+    return tuple(c * LANE for c in counts)
+
+
 def fast_body(activations, cotangent, weights, first_moment, second_moment, *, n, parts):
     depth, cols = weights.shape
     tok, width = activations.shape
     rows = depth // n
-    length, chunks = n // 2, CHUNKS
-    part = rows // chunks
-    sub = part // 4
+    length = n // 2
+    sizes = row_chunks(rows)
+    chunks = len(sizes)
+    sub = LANE // 2
     rounds = parts.bit_length() - 1
     dma = pltpu.SemaphoreType.DMA
     half, full = jnp.bfloat16, jnp.float32
@@ -670,28 +689,30 @@
     anywhere = pl.BlockSpec(memory_space=pl.ANY)
     return tuple(
         pl.pallas_call(
-            functools.partial(fsdp_kernel, n, parts, chunks),
+            functools.partial(fsdp_kernel, n, parts, sizes),
             out_shape=(row, row, row, jax.ShapeDtypeStruct((depth, width), half)),
             in_specs=[anywhere] * 5,
             out_specs=(anywhere,) * 4,
             scratch_shapes=[
-                pltpu.VMEM((2, parts, tok, rows), half),
+                pltpu.VMEM((2, tok, rows), half),
+                pltpu.VMEM((rows, tok), half),
                 pltpu.VMEM((2, parts, rows, tok), half),
                 pltpu.VMEM((2, tok, width), half),
-                pltpu.VMEM((2, 3, part, cols), full),
-                pltpu.VMEM((n, rows, 3 * cols), half),
-                pltpu.VMEM((n, rows, 3 * cols), half),
-                pltpu.VMEM((length, rows, 3 * cols), half),
-                pltpu.VMEM((chunks, hops, part, width), half),
-                pltpu.VMEM((chunks, hops, part, width), half),
-                pltpu.VMEM((part, width), full),
+                pltpu.VMEM((2, 3, cols, rows), full),
+                pltpu.VMEM((n, 3 * cols, rows), half),
+                pltpu.VMEM((n, 3 * cols, rows), half),
+                pltpu.VMEM((length, 3 * cols, rows), half),
+                pltpu.VMEM((hops, rows, width), half),
+                pltpu.VMEM((hops, rows, width), half),
+                pltpu.VMEM((max(sizes), width), full),
+                pltpu.VMEM((3, max(sizes), width), half),
                 pltpu.VMEM((2, 3, sub, width), full),
-                pltpu.VMEM((chunks, part, width), half),
-                dma((2,)), dma((2, 3)), dma((2, 3)), dma((chunks,)),
-                dma, dma, dma, dma,
+                pltpu.VMEM((rows, width), half),
+                dma((2,)), dma, dma((2, 3)), dma((2, 3)), dma((chunks,)),
+                dma, dma, dma((2,)), dma((2,)),
                 dma((2, rounds, parts)), dma((2, parts)),
             ]
-            + [dma((chunks, length))] * 6
+            + [dma((length,))] * 6
             + [dma((chunks, hops))] * 4
             + [dma((chunks, length))] * 2
             + [dma((chunks, hops))] * 4,
@@ -699,7 +720,7 @@
                 collective_id=0, has_side_effects=True, vmem_limit_bytes=67043328
             ),
             name="fsdp_step",
-        )(activations, cotangent, weights, first_moment, second_moment)
+        )(activations, cotangent, weights.T, first_moment.T, second_moment.T)
     )
 
 
@@ -708,8 +729,8 @@
 
     def run(*arrays):
         rows, width = arrays[2].shape[0] // n, arrays[0].shape[1]
-        fits = rows % LANE == 0 and rows % (64 * CHUNKS) == 0 and n == 2 * parts
-        if fits and width == 2 * rows and parts & (parts - 1) == 0:
+        fits = rows % LANE == 0 and n == 2 * parts and width == 2 * rows
+        if fits and arrays[2].shape[1] % 16 == 0 and parts & (parts - 1) == 0:
             return fast_body(*arrays, n=n, parts=parts)
         return body(*arrays, n=n, parts=parts)
 

time: 362 us -> 315 us (0.87)
  Pallas kernels: 329 us -> 297 us
  local copies, waits for them, and re-layouts: 32.2 us -> 17.4 us
    pallas_call x1, Pallas kernels: 329 us -> 297 us  [fast_body(): pl.pallas_call(functools.partial(fsdp_kernel, n, parts, sizes), out_shape...]
    unnamed x11 -> x6, local copies, waits for them, and re-layouts: 32.2 us -> 17.4 us
where the time goes in v1:
time: 315 us
  Pallas kernels  297 us (94%)
  local copies, waits for them, and re-layouts  17.4 us (6%)
    pallas_call x1, Pallas kernels, fast_body(): pl.pallas_call(functools.partial(fsdp_kernel, n, parts, sizes), out_shape...  297 us
    unnamed x6, local copies, waits for them, and re-layouts  17.4 us

profile of v1, /device:TPU:0, one launch (start us, length us, event | category | flops | bytes accessed | tf_op | source)
XLA Modules:
  0.0 314.8 jit_solution(8035560114033219267)
XLA Ops:
  0.6 296.7 %fsdp_step.1 = (f32[640,1280]{1,0:T(8,128)}, f32[640,1280]{1,0:T(8,128)}, f32[640,1280]{1,0:T(8,128)}, bf16[5120,1280]{1,0:T(8,128)(2,1)}) custom-call(bf16[1024,1280]{1,0:T(8,128)(2,1)} %act.1, bf16[1024,1280]{1,0:T(8,128)(2,1)} %cot.1, f32[160,5120]{1,0:T(8,128)} %bitcast.3, f32[160,5120]{1,0:T(8,128)} %bitcast.4, f32[160,5120]{1,0:T(8,128)} %bitcast.5), custom_call_target="tpu_custom_call" | custom-call | tf_op jit(solution)/shard_map/fsdp_step/pallas_call | solution.py:691
  297.4 0.0 copy-start
  297.4 4.0 %copy.13 = f32[640,1280]{1,0:T(8,128)} copy(f32[640,1280]{1,0:T(8,128)} %get-tuple-element.8) | data formatting | bytes 6553600
  301.4 4.6 %copy.14 = f32[640,1280]{1,0:T(8,128)} copy(f32[640,1280]{1,0:T(8,128)} %get-tuple-element.9) | data formatting | bytes 6553600
  306.0 3.8 %copy.15 = f32[640,1280]{1,0:T(8,128)} copy(f32[640,1280]{1,0:T(8,128)} %get-tuple-element.10) | data formatting | bytes 6553600
  309.8 0.0 copy-done
  309.8 4.9 %copy.16 = bf16[5120,1280]{1,0:T(8,128)(2,1)} copy(bf16[5120,1280]{1,0:T(8,128)(2,1)S(1)} %copy-done) | data formatting | bytes 26214400
Async XLA Ops:
  297.4 12.4 %copy-start = (bf16[5120,1280]{1,0:T(8,128)(2,1)S(1)}, bf16[5120,1280]{1,0:T(8,128)(2,1)}, u32[]{:S(2)}) copy-start(bf16[5120,1280]{1,0:T(8,128)(2,1)} %get-tuple-element.11) | copy-start | bytes 39321604

commit v2 on v1

--- a/solution.py
+++ b/solution.py
@@ -231,11 +231,11 @@
 
 
 def fsdp_kernel(
-    n, parts, sizes, act, cot, w_in, m_in, v_in, w_out, m_out, v_out, b_out,
-    raw, give_t, at_buf, c_buf, st_in, st_out, fin, stg, up, dn, tmp, old, stage, wb,
-    raw_sem, loc_sem, st_sem, out_sem, own_sem, give_s, give_r, cot_s, cot_r,
+    n, parts, sizes, batches, relays, order, act, cot, w_in, m_in, v_in, w_out, m_out, v_out, b_out,
+    raw, give_t, at_buf, c_buf, st_in, st_out, fin, stg, up, dn, tmp, old, wb,
+    raw_sem, loc_sem, st_sem, own_sem, give_s, give_r, cot_s, cot_r,
     t_send, t_recv, fin_s, fin_r, stg_s, stg_r, fwd_s, fwd_r,
-    up_s, up_r, dn_s, dn_r, y_send, y_recv, r_send, r_recv, l_send, l_recv,
+    up_s, up_r, dn_s, dn_r, y_send, y_recv, r_send, r_recv, l_send, l_recv, x_send, x_recv,
 ):
     f = lax.axis_index("fsdp")
     t = lax.axis_index("tensor")
@@ -278,16 +278,22 @@
     here = pltpu.make_async_copy(cot, c_buf.at[0], loc_sem)
     here.start()
 
-    def load_state(u, slot):
+    firsts = [sum(batches[:i]) for i in range(len(batches))]
+
+    def batch(i):
+        return pl.ds(firsts[i], batches[i])
+
+    def load_state(i, u, slot):
         d = 2 * ring(u + 1) + (p + 1 + u // length) % 2
+        at = pl.ds(pl.multiple_of(d * rows + firsts[i], LANE), batches[i])
         return [
             pltpu.make_async_copy(
-                src.at[:, lanes(d, rows)], st_in.at[slot, a], st_sem.at[slot, a]
+                src.at[:, at], st_in.at[slot, a, :, pl.ds(0, batches[i])], st_sem.at[slot, a]
             )
             for a, src in enumerate((w_in, m_in, v_in))
         ]
 
-    for c in load_state(0, 0):
+    for c in load_state(0, 0, 0):
         c.start()
 
     barrier = pltpu.get_barrier_semaphore()
@@ -345,7 +351,56 @@
             for h in held(i):
                 block_copy(which, i, h).wait_send()
 
+    def fin_copy(i, zs, zd):
+        return copy(
+            st_out.at[2 * zd + p, :, batch(i)], fin.at[2 * zs + p, :, batch(i)],
+            fin_s.at[i, zd], fin_r.at[i, zs], "fsdp", 2 * zd + p,
+        )
+
+    def stg_copy(i, zs, zd):
+        return copy(
+            st_out.at[2 * zd + 1 - p, :, batch(i)], stg.at[zs, :, batch(i)],
+            stg_s.at[i, zd], stg_r.at[i, zs], "fsdp", 2 * zd + p,
+        )
+
+    def pack(i, u, carry):
+        slot = u % 2
+
+        @pl.when(u + 1 < n)
+        def _():
+            for c in load_state(i, u + 1, (u + 1) % 2):
+                c.start()
+
+        for c in load_state(i, u, slot):
+            c.wait()
+        zd, q = ring(u + 1), (p + 1 + u // length) % 2
+        d = 2 * zd + q
+        for a in range(3):
+            st_out[d, a * cols : (a + 1) * cols, batch(i)] = st_in[
+                slot, a, :, : batches[i]
+            ].astype(jnp.bfloat16)
+
+        @pl.when(d == f)
+        def _():
+            fin[d, :, batch(i)] = st_out[d, :, batch(i)]
+
+        @pl.when((zd != z) & (q == p))
+        def _():
+            fin_copy(i, z, zd).start()
+
+        @pl.when((zd != z) & (q != p))
+        def _():
+            stg_copy(i, z, zd).start()
+
+        return carry
+
     cot_copy(0).start()
+    for i in range(len(batches)):
+        if i:
+            for c in load_state(i, 0, 0):
+                c.start()
+        lax.fori_loop(0, n, functools.partial(pack, i), 0)
+
     raw_copies[0].wait()
     turn(raw.at[0], give_t)
     give = copy(give_t, at_buf.at[1, t], give_s, give_r, "fsdp", pair)
@@ -354,49 +409,6 @@
     raw_copies[1].wait()
     turn(raw.at[1], at_buf.at[0, t])
     spread_own(0)
-
-    def fin_copy(zs, zd):
-        return copy(
-            st_out.at[2 * zd + p], fin.at[2 * zs + p], fin_s.at[zd], fin_r.at[zs],
-            "fsdp", 2 * zd + p,
-        )
-
-    def stg_copy(zs, zd):
-        return copy(
-            st_out.at[2 * zd + 1 - p], stg.at[zs], stg_s.at[zd], stg_r.at[zs],
-            "fsdp", 2 * zd + p,
-        )
-
-    def pack(u, carry):
-        slot = u % 2
-
-        @pl.when(u + 1 < n)
-        def _():
-            for c in load_state(u + 1, (u + 1) % 2):
-                c.start()
-
-        for c in load_state(u, slot):
-            c.wait()
-        zd, q = ring(u + 1), (p + 1 + u // length) % 2
-        d = 2 * zd + q
-        for a in range(3):
-            st_out[d, a * cols : (a + 1) * cols, :] = st_in[slot, a].astype(jnp.bfloat16)
-
-        @pl.when(d == f)
-        def _():
-            fin[d] = st_out[d]
-
-        @pl.when((zd != z) & (q == p))
-        def _():
-            fin_copy(z, zd).start()
-
-        @pl.when((zd != z) & (q != p))
-        def _():
-            stg_copy(z, zd).start()
-
-        return carry
-
-    lax.fori_loop(0, n, pack, 0)
 
     for i in range(len(bits)):
         spread_round(0, i)
@@ -408,25 +420,31 @@
     for i in range(2):
         cot_copy(i).wait_recv()
 
-    def forward(zs, src=None):
-        src = stg.at[zs] if src is None else src
-        return copy(src, fin.at[2 * zs + p], fwd_s.at[zs], fwd_r.at[zs], "fsdp", pair)
-
-    def forward_state(j):
-        zs = ring(length - j)
-        stg_copy(zs, z).wait_recv()
-        forward(zs).start()
-
-    def state_here():
+    def forward(i, zs, src=None):
+        src = stg.at[zs, :, batch(i)] if src is None else src
+        return copy(
+            src, fin.at[2 * zs + p, :, batch(i)], fwd_s.at[i, zs], fwd_r.at[i, zs], "fsdp", pair
+        )
+
+    def forward_state(j, i):
+        if j:
+            zs = ring(length - j)
+            stg_copy(i, zs, z).wait_recv()
+            forward(i, zs).start()
+        else:
+            forward(i, z, st_out.at[pair, :, batch(i)]).start()
+
+    def state_here(i):
         for j in range(1, length):
-            fin_copy(ring(j), z).wait_recv()
+            fin_copy(i, ring(j), z).wait_recv()
         for zs in range(length):
-            got = fin.at[2 * zs + 1 - p]
-            copy(stg.at[zs], got, fwd_s.at[zs], fwd_r.at[zs], "fsdp", pair).wait_recv()
+            got = fin.at[2 * zs + 1 - p, :, batch(i)]
+            forward_here = copy(got, got, fwd_s.at[i, zs], fwd_r.at[i, zs], "fsdp", pair)
+            forward_here.wait_recv()
 
     def term(d, k):
         def tile(i, carry):
-            at = lanes(i, 2 * LANE)
+            at = lanes(i, width // 2)
             tmp[: sizes[k], at] = sum(
                 jnp.dot(
                     at_buf[b, d, span(k), :], c_buf[b, :, at],
@@ -436,7 +454,7 @@
             )
             return carry
 
-        lax.fori_loop(0, width // (2 * LANE), tile, 0)
+        lax.fori_loop(0, 2, tile, 0)
 
     def send_up(k, s):
         slot = s - jnp.minimum(z, 1)
@@ -495,18 +513,16 @@
             add_in(dn, k, s - jnp.minimum(last - z, 1), z == last)
             send_dn(k, s).start()
 
-    sub = stage.shape[2]
-
-    def out_copies(i, slot):
-        return [
-            pltpu.make_async_copy(stage.at[slot, a], dst.at[lanes(i, sub)], out_sem.at[slot, a])
-            for a, dst in enumerate((w_out, m_out, v_out))
-        ]
+    sub = LANE // 2
+
+    arrived = []
 
     def adam(k):
         term(z, k)
-        if k == 0:
-            state_here()
+        for i in range(len(batches)):
+            if i not in arrived and firsts[i] < starts[k] + sizes[k]:
+                state_here(i)
+                arrived.append(i)
 
         def spin(i, carry):
             at = pl.ds(pl.multiple_of(starts[k] + i * LANE, LANE), LANE)
@@ -529,25 +545,17 @@
             tmp[mine, :] += dn[last - 1, span(k), :].astype(jnp.float32)
 
         def piece(j, carry):
-            i = starts[k] // sub + j
-            slot = i % 2
-
-            @pl.when(i >= 2)
-            def _():
-                for c in out_copies(i - 2, slot):
-                    c.wait()
-
+            to = lanes(starts[k] // sub + j, sub)
             at = lanes(j, sub)
             held_now = [old[a, at, :].astype(jnp.float32) for a in range(3)]
             new = adam_update(*held_now, tmp[at, :])
-            for a in range(3):
-                stage[slot, a] = new[a]
-            wb[lanes(i, sub), :] = new[0].astype(jnp.bfloat16)
-            for c in out_copies(i, slot):
-                c.start()
+            for a, out in enumerate((w_out, m_out, v_out)):
+                out[to, :] = new[a]
+            wb[to, :] = new[0].astype(jnp.bfloat16)
             return carry
 
         lax.fori_loop(0, sizes[k] // sub, piece, 0)
+        gather_start(k)
 
     def block(c, q, k):
         return b_out.at[pl.ds(pl.multiple_of((2 * c + q) * rows + starts[k], LANE), sizes[k])]
@@ -580,6 +588,27 @@
             to_left(k, 0, mine).start()
 
         keep(k).start()
+
+    even = z % 2 == 0
+    beside = z + 1 - 2 * (z % 2)
+
+    def relay(k):
+        got = block(z, 1 - p, k)
+        copy(got, got, y_send.at[k, z], y_recv.at[k, z], "fsdp", pair).wait_recv()
+        relay_copy(k, z).start()
+
+    def relay_copy(k, c):
+        got = block(c, 1 - p, k)
+        return copy(got, got, x_send.at[k], x_recv.at[k], "fsdp", 2 * beside + p)
+
+    def onward(k, s, c, near):
+        if s or k not in relays:
+            to_pair(k, c).start()
+        else:
+
+            @pl.when(jnp.logical_not(near))
+            def _():
+                to_pair(k, c).start()
 
     def gather_step(k, s):
         @pl.when(z > s)
@@ -593,7 +622,7 @@
                 def _():
                     to_right(k, s + 1).start()
 
-            to_pair(k, c).start()
+            onward(k, s, c, z % 2 == 1)
 
         @pl.when(z < last - s)
         def _():
@@ -606,41 +635,25 @@
                 def _():
                     to_left(k, s + 1).start()
 
-            to_pair(k, c).start()
-
-    forward(z, st_out.at[pair]).start()
-    waiting = []
-    for s in range(last):
-        reduce_step(0, s)
-        forward_state(s + 1)
-    for k in range(1, len(sizes)):
-        reduce_step(k, 0)
-        adam(k - 1)
-        gather_start(k - 1)
-        for g in waiting:
-            gather_step(*g)
-        waiting = [(k - 1, s) for s in range(last)]
-        for s in range(1, last):
-            reduce_step(k, s)
-            gather_step(*waiting.pop(0))
-    adam(len(sizes) - 1)
-    gather_start(len(sizes) - 1)
-    for g in waiting + [(len(sizes) - 1, s) for s in range(last)]:
-        gather_step(*g)
+            onward(k, s, c, even)
+
+
+    forward_state(0, 0)
+    for kind, *at in order:
+        {
+            "F": forward_state, "R": reduce_step, "A": adam, "G": gather_step, "X": relay,
+        }[kind](*at)
 
     give.wait_send()
     for i in range(2):
         cot_copy(i).wait_send()
         spread_done(i)
-    pieces = rows // sub
-    for j in (2, 1):
-        for c in out_copies(pieces - j, (pieces - j) % 2):
-            c.wait()
-    for j in range(1, length):
-        fin_copy(z, ring(j)).wait_send()
-        stg_copy(z, ring(j)).wait_send()
-    for zs in range(length):
-        forward(zs).wait_send()
+    for i in range(len(batches)):
+        for j in range(1, length):
+            fin_copy(i, z, ring(j)).wait_send()
+            stg_copy(i, z, ring(j)).wait_send()
+        for zs in range(length):
+            forward(i, zs).wait_send()
     for k in range(len(sizes)):
         keep(k).wait()
         for s in range(last):
@@ -661,16 +674,53 @@
             def _():
                 to_left(k, s).wait_send()
 
-        for c in range(length):
+        if k in relays:
+            relay_copy(k, z).wait_send()
+            relay_copy(k, beside).wait_recv()
+            to_pair(k, z).wait_send()
+            others = [ring(j) for j in range(1, length)]
+        else:
+            others = list(range(length))
+
+        def settle(c):
             to_pair(k, c).wait_send()
             theirs = block(c, 1 - p, k)
             copy(theirs, theirs, y_send.at[k, c], y_recv.at[k, c], "fsdp", pair).wait_recv()
 
-
-def row_chunks(rows):
-    tiles = rows // LANE
-    counts = [2] * (tiles // 2) + [1] * (tiles % 2)
-    return tuple(c * LANE for c in counts)
+        for c in others:
+            if k in relays:
+                pl.when(c != beside)(functools.partial(settle, c))
+            else:
+                settle(c)
+
+
+TUNED = (
+    "F01 R00 F30 R01",
+    "F10 F20 R10 F31",
+    "R02 F11 R20 A0",
+    "R11 F21 G00 R12",
+    "R30 G01 R21 A1",
+    "G02 R22 R40 G10",
+    "R31 A2 G11 R32",
+    "G20 G12 R41 A3",
+    "G21 R42 G30 G22",
+    "A4 G31 G40 G32",
+    "G41 X0 G42 X1",
+)
+RELAYS = (0, 1)
+FIRST_BATCH = 1
+
+
+def step_order(chunks, last):
+    if (chunks, last) == (5, 3):
+        order = [(w[0], *(int(c) for c in w[1:])) for w in " ".join(TUNED).split()]
+        first = FIRST_BATCH
+        return tuple(order), RELAYS, (first, chunks - first) if first < chunks else (chunks,)
+    order = [("F", j + 1, 0) for j in range(last)]
+    for k in range(chunks):
+        order += [("R", k, s) for s in range(last)] + [("A", k)]
+        order += [("G", k, s) for s in range(last)]
+    return tuple(order), (), (chunks,)
 
 
 def fast_body(activations, cotangent, weights, first_moment, second_moment, *, n, parts):
@@ -678,21 +728,22 @@
     tok, width = activations.shape
     rows = depth // n
     length = n // 2
-    sizes = row_chunks(rows)
+    sizes = (LANE,) * (rows // LANE)
     chunks = len(sizes)
-    sub = LANE // 2
+    order, relays, batches = step_order(chunks, length - 1)
+    batches = tuple(b * LANE for b in batches)
     rounds = parts.bit_length() - 1
     dma = pltpu.SemaphoreType.DMA
     half, full = jnp.bfloat16, jnp.float32
     hops = max(length - 1, 1)
-    row = jax.ShapeDtypeStruct((rows, width), full)
+    row = pltpu.VMEM((rows, width), full)
     anywhere = pl.BlockSpec(memory_space=pl.ANY)
     return tuple(
         pl.pallas_call(
-            functools.partial(fsdp_kernel, n, parts, sizes),
+            functools.partial(fsdp_kernel, n, parts, sizes, batches, relays, order),
             out_shape=(row, row, row, jax.ShapeDtypeStruct((depth, width), half)),
             in_specs=[anywhere] * 5,
-            out_specs=(anywhere,) * 4,
+            out_specs=(pl.BlockSpec(memory_space=pltpu.VMEM),) * 3 + (anywhere,),
             scratch_shapes=[
                 pltpu.VMEM((2, tok, rows), half),
                 pltpu.VMEM((rows, tok), half),
@@ -706,18 +757,18 @@
                 pltpu.VMEM((hops, rows, width), half),
                 pltpu.VMEM((max(sizes), width), full),
                 pltpu.VMEM((3, max(sizes), width), half),
-                pltpu.VMEM((2, 3, sub, width), full),
                 pltpu.VMEM((rows, width), half),
-                dma((2,)), dma, dma((2, 3)), dma((2, 3)), dma((chunks,)),
+                dma((2,)), dma, dma((2, 3)), dma((chunks,)),
                 dma, dma, dma((2,)), dma((2,)),
                 dma((2, rounds, parts)), dma((2, parts)),
             ]
-            + [dma((length,))] * 6
+            + [dma((len(batches), length))] * 6
             + [dma((chunks, hops))] * 4
             + [dma((chunks, length))] * 2
-            + [dma((chunks, hops))] * 4,
+            + [dma((chunks, hops))] * 4
+            + [dma((chunks,))] * 2,
             compiler_params=pltpu.CompilerParams(
-                collective_id=0, has_side_effects=True, vmem_limit_bytes=67043328
+                collective_id=0, has_side_effects=True, vmem_limit_bytes=54 * 2**20
             ),
             name="fsdp_step",
         )(activations, cotangent, weights.T, first_moment.T, second_moment.T)

time: 315 us -> 297 us (0.943)
  Pallas kernels: 297 us -> 283 us
  local copies, waits for them, and re-layouts: 17.4 us -> 13.2 us
    pallas_call x1, Pallas kernels: 297 us -> 283 us  [fast_body(): pl.pallas_call(functools.partial(fsdp_kernel, n, parts, sizes, batches, r...]
    unnamed x6, local copies, waits for them, and re-layouts: 17.4 us -> 13.2 us
where the time goes in v2:
time: 297 us
  Pallas kernels  283 us (95%)
  local copies, waits for them, and re-layouts  13.2 us (4%)
    pallas_call x1, Pallas kernels, fast_body(): pl.pallas_call(functools.partial(fsdp_kernel, n, parts, sizes, batches, r...  283 us
    unnamed x6, local copies, waits for them, and re-layouts  13.2 us

profile of v2, /device:TPU:0, one launch (start us, length us, event | category | flops | bytes accessed | tf_op | source)
XLA Modules:
  0.0 296.8 jit_solution(520736626428461729)
XLA Ops:
  0.6 283.0 %fsdp_step.1 = (f32[640,1280]{1,0:T(8,128)S(1)}, f32[640,1280]{1,0:T(8,128)S(1)}, f32[640,1280]{1,0:T(8,128)S(1)}, bf16[5120,1280]{1,0:T(8,128)(2,1)}) custom-call(bf16[1024,1280]{1,0:T(8,128)(2,1)} %act.1, bf16[1024,1280]{1,0:T(8,128)(2,1)} %cot.1, f32[160,5120]{1,0:T(8,128)} %bitcast.3, f32[160,5120]{1,0:T(8,128)} %bitcast.4, f32[160,5120]{1,0:T(8,128)} %bitcast.5), custom_call_target="tpu_custom_call" | custom-call | tf_op jit(solution)/shard_map/fsdp_step/pallas_call | solution.py:742
  283.6 0.0 copy-start
  283.6 1.7 copy.13
  285.3 1.7 copy.14
  287.0 1.7 copy.15
  288.7 3.1 %copy-done = bf16[5120,1280]{1,0:T(8,128)(2,1)S(1)} copy-done((bf16[5120,1280]{1,0:T(8,128)(2,1)S(1)}, bf16[5120,1280]{1,0:T(8,128)(2,1)}, u32[]{:S(2)}) %copy-start) | copy-done | bytes 13107224
  291.9 4.9 %copy.16 = bf16[5120,1280]{1,0:T(8,128)(2,1)} copy(bf16[5120,1280]{1,0:T(8,128)(2,1)S(1)} %copy-done) | data formatting | bytes 26214400
Async XLA Ops:
  283.6 8.3 %copy-start = (bf16[5120,1280]{1,0:T(8,128)(2,1)S(1)}, bf16[5120,1280]{1,0:T(8,128)(2,1)}, u32[]{:S(2)}) copy-start(bf16[5120,1280]{1,0:T(8,128)(2,1)} %get-tuple-element.15) | copy-start | bytes 39321604

commit v3 on v2

--- a/solution.py
+++ b/solution.py
@@ -524,14 +524,12 @@
                 state_here(i)
                 arrived.append(i)
 
-        def spin(i, carry):
-            at = pl.ds(pl.multiple_of(starts[k] + i * LANE, LANE), LANE)
+        inset = starts[k] % LANE
+        if not inset:
+            at = pl.ds(starts[k], LANE)
             for a in range(3):
                 parts_of = [fin[src, a * cols : (a + 1) * cols, at] for src in range(n)]
-                old[a, lanes(i, LANE), :] = jnp.concatenate(parts_of, axis=0).T
-            return carry
-
-        lax.fori_loop(0, sizes[k] // LANE, spin, 0)
+                old[a] = jnp.concatenate(parts_of, axis=0).T
         mine = pl.ds(0, sizes[k])
 
         @pl.when(z > 0)
@@ -547,7 +545,8 @@
         def piece(j, carry):
             to = lanes(starts[k] // sub + j, sub)
             at = lanes(j, sub)
-            held_now = [old[a, at, :].astype(jnp.float32) for a in range(3)]
+            was = pl.ds(pl.multiple_of(inset + j * sub, sub), sub)
+            held_now = [old[a, was, :].astype(jnp.float32) for a in range(3)]
             new = adam_update(*held_now, tmp[at, :])
             for a, out in enumerate((w_out, m_out, v_out)):
                 out[to, :] = new[a]
@@ -558,7 +557,7 @@
         gather_start(k)
 
     def block(c, q, k):
-        return b_out.at[pl.ds(pl.multiple_of((2 * c + q) * rows + starts[k], LANE), sizes[k])]
+        return b_out.at[pl.ds(pl.multiple_of((2 * c + q) * rows + starts[k], LANE // 2), sizes[k])]
 
     def to_pair(k, c, src=None):
         src = block(c, p, k) if src is None else src
@@ -695,32 +694,35 @@
 
 
 TUNED = (
-    "F01 R00 F30 R01",
-    "F10 F20 R10 F31",
-    "R02 F11 R20 A0",
-    "R11 F21 G00 R12",
-    "R30 G01 R21 A1",
-    "G02 R22 R40 G10",
-    "R31 A2 G11 R32",
-    "G20 G12 R41 A3",
-    "G21 R42 G30 G22",
-    "A4 G31 G40 G32",
-    "G41 X0 G42 X1",
+    "F21 F31 F10 R00",
+    "F30 F11 R10 R20",
+    "R01 R11 R21 F20",
+    "R02 R12 F01 R22",
+    "A0 A1 A2 G00",
+    "G10 G20 G01 R30",
+    "R31 G11 R50 R40",
+    "G21 G02 R41 G12",
+    "R32 R51 R42 G22",
+    "A3 A4 R52 G40",
+    "G30 A5 G41 G31",
+    "G50 G42 X5 G32",
+    "G51 X2 G52",
 )
-RELAYS = (0, 1)
+RELAYS = (2, 5)
 FIRST_BATCH = 1
 
 
 def step_order(chunks, last):
-    if (chunks, last) == (5, 3):
+    tiles = chunks - 1
+    if (tiles, last) == (5, 3):
         order = [(w[0], *(int(c) for c in w[1:])) for w in " ".join(TUNED).split()]
         first = FIRST_BATCH
-        return tuple(order), RELAYS, (first, chunks - first) if first < chunks else (chunks,)
+        return tuple(order), RELAYS, (first, tiles - first)
     order = [("F", j + 1, 0) for j in range(last)]
     for k in range(chunks):
         order += [("R", k, s) for s in range(last)] + [("A", k)]
         order += [("G", k, s) for s in range(last)]
-    return tuple(order), (), (chunks,)
+    return tuple(order), (), (tiles,)
 
 
 def fast_body(activations, cotangent, weights, first_moment, second_moment, *, n, parts):
@@ -728,7 +730,7 @@
     tok, width = activations.shape
     rows = depth // n
     length = n // 2
-    sizes = (LANE,) * (rows // LANE)
+    sizes = (LANE,) * (rows // LANE - 1) + (LANE // 2,) * 2
     chunks = len(sizes)
     order, relays, batches = step_order(chunks, length - 1)
     batches = tuple(b * LANE for b in batches)

time: 297 us -> 293 us (0.987)
  Pallas kernels: 283 us -> 279 us
    pallas_call x1, Pallas kernels: 283 us -> 279 us  [fast_body(): pl.pallas_call(functools.partial(fsdp_kernel, n, parts, sizes, batches, r...]
where the time goes in v3:
time: 293 us
  Pallas kernels  279 us (95%)
  local copies, waits for them, and re-layouts  13.2 us (5%)
    pallas_call x1, Pallas kernels, fast_body(): pl.pallas_call(functools.partial(fsdp_kernel, n, parts, sizes, batches, r...  279 us
    unnamed x6, local copies, waits for them, and re-layouts  13.2 us

profile of v3, /device:TPU:0, one launch (start us, length us, event | category | flops | bytes accessed | tf_op | source)
XLA Modules:
  0.0 292.5 jit_solution(17687917905976063862)
XLA Ops:
  0.6 278.7 %fsdp_step.1 = (f32[640,1280]{1,0:T(8,128)S(1)}, f32[640,1280]{1,0:T(8,128)S(1)}, f32[640,1280]{1,0:T(8,128)S(1)}, bf16[5120,1280]{1,0:T(8,128)(2,1)}) custom-call(bf16[1024,1280]{1,0:T(8,128)(2,1)} %act.1, bf16[1024,1280]{1,0:T(8,128)(2,1)} %cot.1, f32[160,5120]{1,0:T(8,128)} %bitcast.3, f32[160,5120]{1,0:T(8,128)} %bitcast.4, f32[160,5120]{1,0:T(8,128)} %bitcast.5), custom_call_target="tpu_custom_call" | custom-call | tf_op jit(solution)/shard_map/fsdp_step/pallas_call | solution.py:744
  279.3 0.0 copy-start
  279.3 1.7 copy.13
  281.0 1.7 copy.14
  282.7 1.7 copy.15
  284.4 3.1 %copy-done = bf16[5120,1280]{1,0:T(8,128)(2,1)S(1)} copy-done((bf16[5120,1280]{1,0:T(8,128)(2,1)S(1)}, bf16[5120,1280]{1,0:T(8,128)(2,1)}, u32[]{:S(2)}) %copy-start) | copy-done | bytes 13107224
  287.6 4.9 %copy.16 = bf16[5120,1280]{1,0:T(8,128)(2,1)} copy(bf16[5120,1280]{1,0:T(8,128)(2,1)S(1)} %copy-done) | data formatting | bytes 26214400
Async XLA Ops:
  279.3 8.3 %copy-start = (bf16[5120,1280]{1,0:T(8,128)(2,1)S(1)}, bf16[5120,1280]{1,0:T(8,128)(2,1)}, u32[]{:S(2)}) copy-start(bf16[5120,1280]{1,0:T(8,128)(2,1)} %get-tuple-element.15) | copy-start | bytes 39321604
